TPU v7x, 256 devices: a whole 4x4x8 slice. The times are simulated.
256 devices in a mesh: member: 16 (over z, y_hi), band: 16 (over y_lo, x, core).
Axes of the slice: x: 4, y: 4 (y_hi: 2, y_lo: 2; y = y_hi * 2 + y_lo), z: 8, core: 2. Of those that a mesh axis runs over, the one named last changes fastest.
Arguments:
- spectral: float32 [256, 768, 768], P('member', 'band'), parts along dimension 0, may hold values from -6 to 6
- coupling: float32 [16384, 1024], P(('member', 'band')), parts along dimension 0, may hold values from 0.02 to 162, as said below
- quadratic: float32 [16384, 1024], P(('member', 'band')), parts along dimension 0, may hold values from -1.5 to 1.5
Outputs:
- tendency_spectral: float32 [256, 768, 768], P('member', 'band'), parts along dimension 0
There are 16 independent parts, one for each index of `member`. A program takes and returns all parts, laid end to end along the dimension named above; each array names one. Nothing has to cross between parts.
Inputs may be any that keep to these rules, and one draw needn't show every extreme that they name: `coupling`: positive.
All inputs are finite; a program needn't handle non-finite values.
Results may differ from a plain program's by a relative error of at most 0.00008.
Values sent between devices are 32-bit elements; how exact they have to be, the bound alone decides.
A program may use at most 128 MiB of HBM per device.

v0:
```python
import functools
import math

import jax
import jax.numpy as jnp
import numpy as np
from jax import lax
from jax.experimental import pallas as pl
from jax.experimental.pallas import tpu as pltpu
from jax.sharding import PartitionSpec as P

MESH = pl.DeviceIdType.MESH
F32 = jnp.float32
BF16 = jnp.bfloat16
GROUP = 4
LANES = 128


def small_tables(cells, coeffs):
    half = coeffs // 2
    k = np.arange(half)
    q = np.arange(LANES)
    fine = 2.0 * math.pi / cells * (k[:, None] * q[None, :] % cells)
    steps = np.arange(cells // LANES)
    coarse = 2.0 * math.pi / cells * (steps[:, None] * LANES * k[None, :] % cells)
    by_k = np.stack([np.cos(fine), np.sin(fine)])
    by_q = np.stack([np.cos(fine.T), np.sin(fine.T)])
    row = np.stack([np.cos(coarse), np.sin(coarse)])
    column = np.repeat(row[:, :, :8, None], LANES, axis=3)
    return tuple(a.astype(np.float32) for a in (by_k, by_q, row, column))


def split(value):
    high = value.astype(BF16)
    return high, (value - high.astype(F32)).astype(BF16)


def dot3(a_high, a_low, b_high, b_low):
    dot = functools.partial(jnp.dot, preferred_element_type=F32)
    return dot(a_high, b_high) + dot(a_low, b_high) + dot(a_high, b_low)


def kernel(
    n,
    spectral,
    coupling,
    quadratic,
    by_k,
    by_q,
    row,
    column,
    out,
    x_in,
    send1,
    recv1,
    product,
    send2,
    recv2,
    result,
    part_out,
    part_in,
    wide_high,
    wide_low,
    tall_high,
    tall_low,
    gain,
    bend,
    left_high,
    left_low,
    right_high,
    right_low,
    in_sem,
    out_sem,
    send1_sem,
    recv1_sem,
    send2_sem,
    recv2_sem,
    part_send_sem,
    part_recv_sem,
):
    chunks, band, coeffs = x_in.shape[0], send1.shape[2], x_in.shape[2]
    half = coeffs // 2
    rows, cells = coupling.shape
    points = float(cells * cells)
    wide = GROUP * rows
    me = lax.axis_index("band")

    for c in range(chunks):
        pltpu.make_async_copy(spectral.at[c], x_in.at[c], in_sem.at[c]).start()

    barrier = pltpu.get_barrier_semaphore()

    @pl.loop(1, n)
    def _(k):
        pl.semaphore_signal(
            barrier, inc=1, device_id={"band": lax.rem(me + k, n)}, device_id_type=MESH
        )

    for step in range(cells // LANES):
        lanes = pl.ds(step * LANES, LANES)
        cos_q = by_k[0].reshape(half // 8, 8, LANES)
        sin_q = by_k[1].reshape(half // 8, 8, LANES)
        cos_s, sin_s = column[0, step][None], column[1, step][None]
        cosine = (cos_q * cos_s - sin_q * sin_s).reshape(half, LANES)
        sine = (sin_q * cos_s + cos_q * sin_s).reshape(half, LANES)
        wide_high[pl.ds(0, half), lanes], wide_low[pl.ds(0, half), lanes] = split(cosine)
        wide_high[pl.ds(half, half), lanes], wide_low[pl.ds(half, half), lanes] = split(sine)

    pl.semaphore_wait(barrier, n - 1)

    low_half = lax.broadcasted_iota(jnp.int32, (band, LANES), 1) < rows

    def send(source, target, c, send_sem, recv_sem):
        @pl.loop(1, n)
        def _(k):
            other = lax.rem(me + k, n)
            pltpu.make_async_remote_copy(
                src_ref=source.at[c, other],
                dst_ref=target.at[c, me],
                send_sem=send_sem.at[c],
                recv_sem=recv_sem.at[c],
                device_id={"band": other},
                device_id_type=MESH,
            ).start()
        target[c, me] = source[c, me]

    def arrivals(source, target, c, send_sem, recv_sem):
        others = pl.ds(0, n - 1)
        return pltpu.make_async_remote_copy(
            src_ref=source.at[c, others],
            dst_ref=target.at[c, others],
            send_sem=send_sem.at[c],
            recv_sem=recv_sem.at[c],
            device_id={"band": lax.rem(me + 1, n)},
            device_id_type=MESH,
        )

    first = (send1, recv1)
    second = (send2, recv2)

    @pl.loop(0, chunks)
    def _(c):
        pltpu.make_async_copy(spectral.at[c], x_in.at[c], in_sem.at[c]).wait()
        x_high, x_low = split(x_in[c])
        for j in range(cells // wide):
            lanes = pl.ds(j * wide, wide)
            section = dot3(x_high, x_low, wide_high[:, lanes], wide_low[:, lanes])
            for level in range(0, GROUP, 2):
                for t in range(wide // LANES):
                    part = slice(t * LANES, (t + 1) * LANES)
                    even = section[level * band : (level + 1) * band, part]
                    odd = section[(level + 1) * band : (level + 2) * band, part]
                    target = 2 * (j * (wide // LANES) + t)
                    place = pl.ds(level * rows, LANES)
                    send1[c, target, :, place] = jnp.where(
                        low_half, even, pltpu.roll(odd, rows, 1)
                    )
                    send1[c, target + 1, :, place] = jnp.where(
                        low_half, pltpu.roll(even, rows, 1), odd
                    )

        @pl.when(c < 2)
        def _():
            send(*first, c, send1_sem, recv1_sem)

    for step in range(cells // LANES):
        points_here = pl.ds(step * LANES, LANES)
        cos_s, sin_s = row[0, pl.ds(step, 1)], row[1, pl.ds(step, 1)]
        cosine = by_q[0] * cos_s - by_q[1] * sin_s
        sine = by_q[1] * cos_s + by_q[0] * sin_s
        (tall_high[points_here, pl.ds(0, half)], tall_low[points_here, pl.ds(0, half)]) = split(
            cosine
        )
        (
            tall_high[points_here, pl.ds(half, half)],
            tall_low[points_here, pl.ds(half, half)],
        ) = split(sine)

    for step in range(cells // LANES):
        here = pl.ds(step * LANES, LANES)
        field = coupling[:, here] * (1.0 / half)
        gain[here, :] = jnp.concatenate([field, field], axis=0).T
        field = quadratic[:, here]
        bend[here, :] = jnp.concatenate([field, field], axis=0).T

    def synthesize(c):
        arrivals(*first, c, send1_sem, recv1_sem).wait_recv()
        right_high[pl.ds(0, coeffs)], right_low[pl.ds(0, coeffs)] = split(
            recv1[c].reshape(coeffs, wide)
        )
        grid = dot3(
            tall_high[...],
            tall_low[...],
            right_high[pl.ds(0, coeffs)],
            right_low[pl.ds(0, coeffs)],
        )
        for t in range(wide // LANES):
            lanes = slice(t * LANES, (t + 1) * LANES)
            value = gain[...] * grid[:, lanes]
            product[c, :, lanes] = value
            part_out[c, pl.ds(t, 1), :] = jnp.sum(value * value, axis=0, keepdims=True)

        @pl.loop(1, n)
        def _(k):
            other = lax.rem(me + k, n)
            pltpu.make_async_remote_copy(
                src_ref=part_out.at[c],
                dst_ref=part_in.at[c, me],
                send_sem=part_send_sem.at[c],
                recv_sem=part_recv_sem.at[c],
                device_id={"band": other},
                device_id_type=MESH,
            ).start()
        part_in[c, me] = part_out[c]

    def analyze(c):
        others = pl.ds(0, n - 1)
        done = pltpu.make_async_remote_copy(
            src_ref=part_in.at[c, others],
            dst_ref=part_in.at[c, others],
            send_sem=part_send_sem.at[c],
            recv_sem=part_recv_sem.at[c],
            device_id={"band": lax.rem(me + 1, n)},
            device_id_type=MESH,
        )
        done.wait_recv()
        sums = part_in[c, 0]
        for source in range(1, n):
            sums = sums + part_in[c, source]
        left = lax.broadcasted_iota(jnp.int32, sums.shape, 1) < rows
        total = jnp.where(
            left,
            jnp.sum(jnp.where(left, sums, 0.0), axis=1, keepdims=True),
            jnp.sum(jnp.where(left, 0.0, sums), axis=1, keepdims=True),
        )
        scale = 1.0 / jnp.sqrt(total * (1.0 / points) + 1e-06)
        for t in range(wide // LANES):
            lanes = slice(t * LANES, (t + 1) * LANES)
            scaled = product[c, :, lanes] * scale[t : t + 1]
            tendency = scaled + bend[...] * scaled * scaled
            right_high[:, lanes], right_low[:, lanes] = split(tendency)
        back = dot3(wide_high[...], wide_low[...], right_high[...], right_low[...])
        send2[c] = back.reshape(n, band, wide)
        send(*second, c, send2_sem, recv2_sem)

    x_index = lax.broadcasted_iota(jnp.int32, (band, coeffs), 0) + me * band
    y_index = lax.broadcasted_iota(jnp.int32, (band, coeffs), 1)

    def weight(index):
        return jnp.where((index == 0) | (index == half), 1.0, 2.0)

    def finish(c):
        arrivals(*second, c, send2_sem, recv2_sem).wait_recv()
        for level in range(0, GROUP, 2):
            place = pl.ds(level * rows, LANES)
            for t in range(cells // LANES):
                lanes = pl.ds(t * LANES, LANES)
                even = recv2[c, 2 * t, :, place]
                odd = recv2[c, 2 * t + 1, :, place]
                for which, value in (
                    (level, jnp.where(low_half, even, pltpu.roll(odd, rows, 1))),
                    (level + 1, jnp.where(low_half, pltpu.roll(even, rows, 1), odd)),
                ):
                    here = pl.ds(which * band, band)
                    left_high[here, lanes], left_low[here, lanes] = split(value)
        done = dot3(left_high[...], left_low[...], tall_high[...], tall_low[...])
        factor = weight(x_index) * weight(y_index) * (half / points)
        for level in range(GROUP):
            here = slice(level * band, (level + 1) * band)
            result[c, here, :] = done[here] * factor
        pltpu.make_async_copy(result.at[c], out.at[c], out_sem.at[c]).start()

    @pl.loop(0, chunks + 3)
    def _(t):
        @pl.when(t < chunks)
        def _():
            synthesize(t)

        @pl.when(t + 2 < chunks)
        def _():
            send(*first, t + 2, send1_sem, recv1_sem)

        @pl.when((t >= 1) & (t < chunks + 1))
        def _():
            analyze(t - 1)

        @pl.when(t >= 3)
        def _():
            finish(t - 3)

    @pl.loop(0, chunks)
    def _(c):
        arrivals(*first, c, send1_sem, recv1_sem).wait_send()
        arrivals(*second, c, send2_sem, recv2_sem).wait_send()
        others = pl.ds(0, n - 1)
        pltpu.make_async_remote_copy(
            src_ref=part_in.at[c, others],
            dst_ref=part_in.at[c, others],
            send_sem=part_send_sem.at[c],
            recv_sem=part_recv_sem.at[c],
            device_id={"band": lax.rem(me + 1, n)},
            device_id_type=MESH,
        ).wait_send()
        pltpu.make_async_copy(result.at[c], out.at[c], out_sem.at[c]).wait()


def solution(mesh):
    n = mesh.shape["band"]

    def on_device(spectral, coupling, quadratic):
        levels, band, coeffs = spectral.shape
        rows, cells = coupling.shape
        chunks = levels // GROUP
        wide = GROUP * rows
        tables = small_tables(cells, coeffs)
        dma = pltpu.SemaphoreType.DMA
        vmem = pl.BlockSpec(memory_space=pltpu.VMEM)
        hbm = pl.BlockSpec(memory_space=pl.ANY)
        result = pl.pallas_call(
            functools.partial(kernel, n),
            out_shape=jax.ShapeDtypeStruct((chunks, GROUP * band, coeffs), F32),
            in_specs=[hbm] + [vmem] * 6,
            out_specs=hbm,
            scratch_shapes=[
                pltpu.VMEM((chunks, GROUP * band, coeffs), F32),
                pltpu.VMEM((chunks, n, band, wide), F32),
                pltpu.VMEM((chunks, n, band, wide), F32),
                pltpu.VMEM((chunks, cells, wide), F32),
                pltpu.VMEM((chunks, n, band, wide), F32),
                pltpu.VMEM((chunks, n, band, wide), F32),
                pltpu.VMEM((chunks, GROUP * band, coeffs), F32),
                pltpu.VMEM((chunks, wide // LANES, LANES), F32),
                pltpu.VMEM((chunks, n, wide // LANES, LANES), F32),
                pltpu.VMEM((coeffs, cells), BF16),
                pltpu.VMEM((coeffs, cells), BF16),
                pltpu.VMEM((cells, coeffs), BF16),
                pltpu.VMEM((cells, coeffs), BF16),
                pltpu.VMEM((cells, LANES), F32),
                pltpu.VMEM((cells, LANES), F32),
                pltpu.VMEM((GROUP * band, cells), BF16),
                pltpu.VMEM((GROUP * band, cells), BF16),
                pltpu.VMEM((cells, wide), BF16),
                pltpu.VMEM((cells, wide), BF16),
            ]
            + [dma((chunks,))] * 8,
            compiler_params=pltpu.CompilerParams(
                collective_id=0, has_side_effects=True, vmem_limit_bytes=56 * 1024 * 1024
            ),
        )(spectral.reshape(chunks, GROUP * band, coeffs), coupling, quadratic, *tables)
        return result.reshape(levels, band, coeffs)

    spec = P("member", "band", None)
    field = P(("member", "band"), None)
    return jax.shard_map(
        on_device,
        mesh=mesh,
        in_specs=(spec, field, field),
        out_specs=spec,
        check_vma=False,
    )
```

profile of v0, /device:TPU:1, one launch (start us, length us, event | category | flops | bytes accessed | tf_op | source)
XLA Modules:
  0.0 85.7 jit_solution(15054684943958593757)
XLA Ops:
  0.0 82.4 %shard_map.73 = f32[4,192,768]{2,1,0:T(8,128)} custom-call(f32[4,192,768]{2,1,0:T(8,128)} %bitcast.3, f32[64,1024]{1,0:T(8,128)} %coupling.1, f32[64,1024]{1,0:T(8,128)} %quadratic.1, f32[2,384,128]{2,1,0:T(8,128)} %constant.8.clone.by_k, f32[2,128,384]{2,1,0:T(8,128)} %constant.9.clone.by_q, f32[2,8,384]{2,1,0:T(8,128)} %constant.10.clone.row, ...), custom_call_target="tpu_custom_call" | custom-call | tf_op jit(solution)/shard_map/pallas_call | solution.py:319
  82.4 3.2 %copy.9 = f32[16,48,768]{2,1,0:T(8,128)} copy(f32[16,48,768]{2,1,0:T(8,128)} %bitcast.2) | data formatting | bytes 4718592
where the time goes:
time: 85.8 us; the launch traced here: 85.7 us
  Pallas kernels  82.4 us (96%)
  local copies, waits for them, and re-layouts  3.23 us (4%)
    pallas_call x1, Pallas kernels, on_device(): pl.pallas_call(functools.partial(kernel, n), out_shape=jax.ShapeDtypeStru...  82.4 us
    unnamed x1, local copies, waits for them, and re-layouts  3.23 us

commit v1 on v0

--- a/solution.py
+++ b/solution.py
@@ -3,7 +3,6 @@
 
 import jax
 import jax.numpy as jnp
-import numpy as np
 from jax import lax
 from jax.experimental import pallas as pl
 from jax.experimental.pallas import tpu as pltpu
@@ -16,18 +15,30 @@
 LANES = 128
 
 
-def small_tables(cells, coeffs):
-    half = coeffs // 2
-    k = np.arange(half)
-    q = np.arange(LANES)
-    fine = 2.0 * math.pi / cells * (k[:, None] * q[None, :] % cells)
-    steps = np.arange(cells // LANES)
-    coarse = 2.0 * math.pi / cells * (steps[:, None] * LANES * k[None, :] % cells)
-    by_k = np.stack([np.cos(fine), np.sin(fine)])
-    by_q = np.stack([np.cos(fine.T), np.sin(fine.T)])
-    row = np.stack([np.cos(coarse), np.sin(coarse)])
-    column = np.repeat(row[:, :, :8, None], LANES, axis=3)
-    return tuple(a.astype(np.float32) for a in (by_k, by_q, row, column))
+SINE = (-1.6666666666666666e-01, 8.3333333333333333e-03, -1.9841269841269841e-04, 2.7557319223985891e-06)
+COSINE = (-0.5, 4.1666666666666667e-02, -1.3888888888888889e-03, 2.4801587301587302e-05, -2.7557319223985891e-07)
+
+
+def turn(index, cells):
+    quarter = cells // 4
+    index = lax.rem(index, cells)
+    which = index // quarter
+    angle = (index - which * quarter - quarter // 2).astype(F32) * (2.0 * math.pi / cells)
+    square = angle * angle
+
+    def series(terms):
+        total = terms[-1]
+        for term in terms[-2::-1]:
+            total = total * square + term
+        return total * square + 1.0
+
+    cosine = series(COSINE) * math.sqrt(0.5)
+    sine = series(SINE) * angle * math.sqrt(0.5)
+    plus, minus = cosine + sine, cosine - sine
+    cos_sign = jnp.where((which == 1) | (which == 2), -1.0, 1.0)
+    sin_sign = jnp.where(which >= 2, -1.0, 1.0)
+    odd = (which == 1) | (which == 3)
+    return jnp.where(odd, plus, minus) * cos_sign, jnp.where(odd, minus, plus) * sin_sign
 
 
 def split(value):
@@ -43,20 +54,17 @@
 def kernel(
     n,
     spectral,
+    coupling_hbm,
+    quadratic_hbm,
+    out,
+    x_in,
     coupling,
     quadratic,
-    by_k,
-    by_q,
-    row,
-    column,
-    out,
-    x_in,
     send1,
     recv1,
     product,
     send2,
     recv2,
-    result,
     part_out,
     part_in,
     wide_high,
@@ -70,7 +78,7 @@
     right_high,
     right_low,
     in_sem,
-    out_sem,
+    field_sem,
     send1_sem,
     recv1_sem,
     send2_sem,
@@ -87,6 +95,8 @@
 
     for c in range(chunks):
         pltpu.make_async_copy(spectral.at[c], x_in.at[c], in_sem.at[c]).start()
+    pltpu.make_async_copy(coupling_hbm, coupling, field_sem.at[0]).start()
+    pltpu.make_async_copy(quadratic_hbm, quadratic, field_sem.at[1]).start()
 
     barrier = pltpu.get_barrier_semaphore()
 
@@ -96,32 +106,38 @@
             barrier, inc=1, device_id={"band": lax.rem(me + k, n)}, device_id_type=MESH
         )
 
+    def count(shape, axis):
+        return lax.broadcasted_iota(jnp.int32, shape, axis)
+
+    fine = (half, LANES)
+    cos_q, sin_q = turn(count(fine, 0) * count(fine, 1), cells)
+    cos_q = cos_q.reshape(half // 8, 8, LANES)
+    sin_q = sin_q.reshape(half // 8, 8, LANES)
     for step in range(cells // LANES):
         lanes = pl.ds(step * LANES, LANES)
-        cos_q = by_k[0].reshape(half // 8, 8, LANES)
-        sin_q = by_k[1].reshape(half // 8, 8, LANES)
-        cos_s, sin_s = column[0, step][None], column[1, step][None]
+        cos_s, sin_s = turn(count((8, LANES), 0) * (step * LANES), cells)
+        cos_s, sin_s = cos_s[None], sin_s[None]
         cosine = (cos_q * cos_s - sin_q * sin_s).reshape(half, LANES)
         sine = (sin_q * cos_s + cos_q * sin_s).reshape(half, LANES)
         wide_high[pl.ds(0, half), lanes], wide_low[pl.ds(0, half), lanes] = split(cosine)
         wide_high[pl.ds(half, half), lanes], wide_low[pl.ds(half, half), lanes] = split(sine)
 
-    pl.semaphore_wait(barrier, n - 1)
-
     low_half = lax.broadcasted_iota(jnp.int32, (band, LANES), 1) < rows
+
+    def send_one(source, target, c, send_sem, recv_sem, other):
+        pltpu.make_async_remote_copy(
+            src_ref=source.at[c, other],
+            dst_ref=target.at[c, me],
+            send_sem=send_sem.at[c],
+            recv_sem=recv_sem.at[c],
+            device_id={"band": other},
+            device_id_type=MESH,
+        ).start()
 
     def send(source, target, c, send_sem, recv_sem):
         @pl.loop(1, n)
         def _(k):
-            other = lax.rem(me + k, n)
-            pltpu.make_async_remote_copy(
-                src_ref=source.at[c, other],
-                dst_ref=target.at[c, me],
-                send_sem=send_sem.at[c],
-                recv_sem=recv_sem.at[c],
-                device_id={"band": other},
-                device_id_type=MESH,
-            ).start()
+            send_one(source, target, c, send_sem, recv_sem, lax.rem(me + k, n))
         target[c, me] = source[c, me]
 
     def arrivals(source, target, c, send_sem, recv_sem):
@@ -142,15 +158,19 @@
     def _(c):
         pltpu.make_async_copy(spectral.at[c], x_in.at[c], in_sem.at[c]).wait()
         x_high, x_low = split(x_in[c])
-        for j in range(cells // wide):
-            lanes = pl.ds(j * wide, wide)
+        per = wide // rows
+
+        @pl.loop(0, cells // wide)
+        def _(turned):
+            j = lax.rem(turned + me // per + 1, cells // wide)
+            lanes = pl.ds(pl.multiple_of(j * wide, wide), wide)
             section = dot3(x_high, x_low, wide_high[:, lanes], wide_low[:, lanes])
             for level in range(0, GROUP, 2):
                 for t in range(wide // LANES):
                     part = slice(t * LANES, (t + 1) * LANES)
                     even = section[level * band : (level + 1) * band, part]
                     odd = section[(level + 1) * band : (level + 2) * band, part]
-                    target = 2 * (j * (wide // LANES) + t)
+                    target = j * per + 2 * t
                     place = pl.ds(level * rows, LANES)
                     send1[c, target, :, place] = jnp.where(
                         low_half, even, pltpu.roll(odd, rows, 1)
@@ -159,15 +179,32 @@
                         low_half, pltpu.roll(even, rows, 1), odd
                     )
 
+            @pl.when((c == 0) & (turned == 0))
+            def _():
+                pl.semaphore_wait(barrier, n - 1)
+
+            @pl.when(c < 2)
+            def _():
+                @pl.loop(0, per)
+                def _(i):
+                    other = j * per + i
+
+                    @pl.when(other != me)
+                    def _():
+                        send_one(*first, c, send1_sem, recv1_sem, other)
+
         @pl.when(c < 2)
         def _():
-            send(*first, c, send1_sem, recv1_sem)
-
+            recv1[c, me] = send1[c, me]
+
+    fine = (LANES, half)
+    cos_q, sin_q = turn(count(fine, 0) * count(fine, 1), cells)
     for step in range(cells // LANES):
         points_here = pl.ds(step * LANES, LANES)
-        cos_s, sin_s = row[0, pl.ds(step, 1)], row[1, pl.ds(step, 1)]
-        cosine = by_q[0] * cos_s - by_q[1] * sin_s
-        sine = by_q[1] * cos_s + by_q[0] * sin_s
+        cos_s, sin_s = turn(count((8, half), 1) * (step * LANES), cells)
+        cos_s, sin_s = cos_s[:1], sin_s[:1]
+        cosine = cos_q * cos_s - sin_q * sin_s
+        sine = sin_q * cos_s + cos_q * sin_s
         (tall_high[points_here, pl.ds(0, half)], tall_low[points_here, pl.ds(0, half)]) = split(
             cosine
         )
@@ -175,6 +212,9 @@
             tall_high[points_here, pl.ds(half, half)],
             tall_low[points_here, pl.ds(half, half)],
         ) = split(sine)
+
+    pltpu.make_async_copy(coupling_hbm, coupling, field_sem.at[0]).wait()
+    pltpu.make_async_copy(quadratic_hbm, quadratic, field_sem.at[1]).wait()
 
     for step in range(cells // LANES):
         here = pl.ds(step * LANES, LANES)
@@ -267,8 +307,7 @@
         factor = weight(x_index) * weight(y_index) * (half / points)
         for level in range(GROUP):
             here = slice(level * band, (level + 1) * band)
-            result[c, here, :] = done[here] * factor
-        pltpu.make_async_copy(result.at[c], out.at[c], out_sem.at[c]).start()
+            out[c, here, :] = done[here] * factor
 
     @pl.loop(0, chunks + 3)
     def _(t):
@@ -301,7 +340,6 @@
             device_id={"band": lax.rem(me + 1, n)},
             device_id_type=MESH,
         ).wait_send()
-        pltpu.make_async_copy(result.at[c], out.at[c], out_sem.at[c]).wait()
 
 
 def solution(mesh):
@@ -312,23 +350,23 @@
         rows, cells = coupling.shape
         chunks = levels // GROUP
         wide = GROUP * rows
-        tables = small_tables(cells, coeffs)
         dma = pltpu.SemaphoreType.DMA
         vmem = pl.BlockSpec(memory_space=pltpu.VMEM)
-        hbm = pl.BlockSpec(memory_space=pl.ANY)
+        hbm = pl.BlockSpec(memory_space=pltpu.HBM)
         result = pl.pallas_call(
             functools.partial(kernel, n),
-            out_shape=jax.ShapeDtypeStruct((chunks, GROUP * band, coeffs), F32),
-            in_specs=[hbm] + [vmem] * 6,
-            out_specs=hbm,
+            out_shape=pltpu.VMEM((chunks, GROUP * band, coeffs), F32),
+            in_specs=[hbm] * 3,
+            out_specs=vmem,
             scratch_shapes=[
                 pltpu.VMEM((chunks, GROUP * band, coeffs), F32),
+                pltpu.VMEM((rows, cells), F32),
+                pltpu.VMEM((rows, cells), F32),
                 pltpu.VMEM((chunks, n, band, wide), F32),
                 pltpu.VMEM((chunks, n, band, wide), F32),
                 pltpu.VMEM((chunks, cells, wide), F32),
                 pltpu.VMEM((chunks, n, band, wide), F32),
                 pltpu.VMEM((chunks, n, band, wide), F32),
-                pltpu.VMEM((chunks, GROUP * band, coeffs), F32),
                 pltpu.VMEM((chunks, wide // LANES, LANES), F32),
                 pltpu.VMEM((chunks, n, wide // LANES, LANES), F32),
                 pltpu.VMEM((coeffs, cells), BF16),
@@ -342,11 +380,16 @@
                 pltpu.VMEM((cells, wide), BF16),
                 pltpu.VMEM((cells, wide), BF16),
             ]
-            + [dma((chunks,))] * 8,
+            + [dma((chunks,)), dma((2,))] + [dma((chunks,))] * 6,
             compiler_params=pltpu.CompilerParams(
-                collective_id=0, has_side_effects=True, vmem_limit_bytes=56 * 1024 * 1024
+                collective_id=0, has_side_effects=True, vmem_limit_bytes=44 * 1024 * 1024
             ),
-        )(spectral.reshape(chunks, GROUP * band, coeffs), coupling, quadratic, *tables)
+        )(
+            *(
+                pltpu.with_memory_space_constraint(value, pltpu.HBM)
+                for value in (spectral.reshape(chunks, GROUP * band, coeffs), coupling, quadratic)
+            )
+        )
         return result.reshape(levels, band, coeffs)
 
     spec = P("member", "band", None)

time: 85.8 us -> 80.7 us (0.941)
  Pallas kernels: 82.4 us -> 79.3 us
  local copies, waits for them, and re-layouts: 3.23 us -> 1.41 us
    pallas_call x1, Pallas kernels: 82.4 us -> 79.3 us  [on_device(): pl.pallas_call(functools.partial(kernel, n), out_shape=pltpu.VMEM((chunks...]
    unnamed x1, local copies, waits for them, and re-layouts: 3.23 us -> 1.41 us
where the time goes in v1:
time: 80.7 us
  Pallas kernels  79.3 us (98%)
  local copies, waits for them, and re-layouts  1.41 us (2%)
    pallas_call x1, Pallas kernels, on_device(): pl.pallas_call(functools.partial(kernel, n), out_shape=pltpu.VMEM((chunks...  79.3 us

profile of v1, /device:TPU:1, one launch (start us, length us, event | category | flops | bytes accessed | tf_op | source)
XLA Modules:
  0.0 80.7 jit_solution(14454798815906528680)
XLA Ops:
  0.0 79.3 %shard_map.37 = f32[4,192,768]{2,1,0:T(8,128)S(1)} custom-call(f32[4,192,768]{2,1,0:T(8,128)} %bitcast.3, f32[64,1024]{1,0:T(8,128)} %coupling_hbm.1, f32[64,1024]{1,0:T(8,128)} %quadratic_hbm.1), custom_call_target="tpu_custom_call" | custom-call | tf_op jit(solution)/shard_map/pallas_call | solution.py:356
  79.3 1.4 %copy.5 = f32[16,48,768]{2,1,0:T(8,128)} copy(f32[16,48,768]{2,1,0:T(8,128)S(1)} %bitcast.2) | data formatting | bytes 4718592

commit v2 on v1

--- a/solution.py
+++ b/solution.py
@@ -11,8 +11,12 @@
 MESH = pl.DeviceIdType.MESH
 F32 = jnp.float32
 BF16 = jnp.bfloat16
-GROUP = 4
+GROUP = 2
+AHEAD = 3
+ANALYZE = 3
+FINISH = 6
 LANES = 128
+ORDER = ((1, 2), (0, 1), (1, 3), (0, 2), (1, 0), (0, 3), (1, 1), (0, 0))
 
 
 SINE = (-1.6666666666666666e-01, 8.3333333333333333e-03, -1.9841269841269841e-04, 2.7557319223985891e-06)
@@ -77,6 +81,8 @@
     left_low,
     right_high,
     right_low,
+    down_high,
+    down_low,
     in_sem,
     field_sem,
     send1_sem,
@@ -90,8 +96,17 @@
     half = coeffs // 2
     rows, cells = coupling.shape
     points = float(cells * cells)
+    fold = cells // 2
     wide = GROUP * rows
     me = lax.axis_index("band")
+    chip, core = me // 2, lax.rem(me, 2)
+    ring = n // 4
+
+    def at(dy, dx, dc):
+        y, x = lax.rem(chip // ring + dy, 2), lax.rem(chip + dx, ring)
+        return 2 * (ring * y + x) + lax.rem(core + dc, 2)
+
+    others = [at(dy, dx, dc) for dy, dx in ORDER for dc in range(2) if (dy, dx, dc) != (0, 0, 0)]
 
     for c in range(chunks):
         pltpu.make_async_copy(spectral.at[c], x_in.at[c], in_sem.at[c]).start()
@@ -113,7 +128,7 @@
     cos_q, sin_q = turn(count(fine, 0) * count(fine, 1), cells)
     cos_q = cos_q.reshape(half // 8, 8, LANES)
     sin_q = sin_q.reshape(half // 8, 8, LANES)
-    for step in range(cells // LANES):
+    for step in range(fold // LANES):
         lanes = pl.ds(step * LANES, LANES)
         cos_s, sin_s = turn(count((8, LANES), 0) * (step * LANES), cells)
         cos_s, sin_s = cos_s[None], sin_s[None]
@@ -135,16 +150,15 @@
         ).start()
 
     def send(source, target, c, send_sem, recv_sem):
-        @pl.loop(1, n)
-        def _(k):
-            send_one(source, target, c, send_sem, recv_sem, lax.rem(me + k, n))
+        for other in others:
+            send_one(source, target, c, send_sem, recv_sem, other)
         target[c, me] = source[c, me]
 
     def arrivals(source, target, c, send_sem, recv_sem):
-        others = pl.ds(0, n - 1)
+        rest = pl.ds(0, n - 1)
         return pltpu.make_async_remote_copy(
-            src_ref=source.at[c, others],
-            dst_ref=target.at[c, others],
+            src_ref=source.at[c, rest],
+            dst_ref=target.at[c, rest],
             send_sem=send_sem.at[c],
             recv_sem=recv_sem.at[c],
             device_id={"band": lax.rem(me + 1, n)},
@@ -157,49 +171,41 @@
     @pl.loop(0, chunks)
     def _(c):
         pltpu.make_async_copy(spectral.at[c], x_in.at[c], in_sem.at[c]).wait()
-        x_high, x_low = split(x_in[c])
-        per = wide // rows
-
-        @pl.loop(0, cells // wide)
-        def _(turned):
-            j = lax.rem(turned + me // per + 1, cells // wide)
-            lanes = pl.ds(pl.multiple_of(j * wide, wide), wide)
-            section = dot3(x_high, x_low, wide_high[:, lanes], wide_low[:, lanes])
-            for level in range(0, GROUP, 2):
-                for t in range(wide // LANES):
-                    part = slice(t * LANES, (t + 1) * LANES)
-                    even = section[level * band : (level + 1) * band, part]
-                    odd = section[(level + 1) * band : (level + 2) * band, part]
-                    target = j * per + 2 * t
-                    place = pl.ds(level * rows, LANES)
-                    send1[c, target, :, place] = jnp.where(
-                        low_half, even, pltpu.roll(odd, rows, 1)
-                    )
-                    send1[c, target + 1, :, place] = jnp.where(
-                        low_half, pltpu.roll(even, rows, 1), odd
-                    )
-
-            @pl.when((c == 0) & (turned == 0))
-            def _():
-                pl.semaphore_wait(barrier, n - 1)
-
-            @pl.when(c < 2)
-            def _():
-                @pl.loop(0, per)
-                def _(i):
-                    other = j * per + i
-
-                    @pl.when(other != me)
-                    def _():
-                        send_one(*first, c, send1_sem, recv1_sem, other)
-
-        @pl.when(c < 2)
-        def _():
-            recv1[c, me] = send1[c, me]
+        value = x_in[c]
+        even_k = lax.rem(count(value.shape, 1), 2) == 0
+        parts = jnp.concatenate([jnp.where(even_k, value, 0.0), jnp.where(even_k, 0.0, value)])
+        x_high, x_low = split(parts)
+        tile = 2 * LANES
+        for j in range(fold // tile):
+            lanes = pl.ds(j * tile, tile)
+            both = dot3(x_high, x_low, wide_high[:, lanes], wide_low[:, lanes])
+            even_sum, odd_sum = both[: GROUP * band], both[GROUP * band :]
+            for side, section in enumerate((even_sum + odd_sum, even_sum - odd_sum)):
+                for level in range(0, GROUP, 2):
+                    for t in range(tile // LANES):
+                        part = slice(t * LANES, (t + 1) * LANES)
+                        even = section[level * band : (level + 1) * band, part]
+                        odd = section[(level + 1) * band : (level + 2) * band, part]
+                        target = (side * fold + j * tile + t * LANES) // rows
+                        place = pl.ds(level * rows, LANES)
+                        send1[c, target, :, place] = jnp.where(
+                            low_half, even, pltpu.roll(odd, rows, 1)
+                        )
+                        send1[c, target + 1, :, place] = jnp.where(
+                            low_half, pltpu.roll(even, rows, 1), odd
+                        )
+
+        @pl.when(c == 0)
+        def _():
+            pl.semaphore_wait(barrier, n - 1)
+
+        @pl.when(c < AHEAD)
+        def _():
+            send(*first, c, send1_sem, recv1_sem)
 
     fine = (LANES, half)
     cos_q, sin_q = turn(count(fine, 0) * count(fine, 1), cells)
-    for step in range(cells // LANES):
+    for step in range(fold // LANES):
         points_here = pl.ds(step * LANES, LANES)
         cos_s, sin_s = turn(count((8, half), 1) * (step * LANES), cells)
         cos_s, sin_s = cos_s[:1], sin_s[:1]
@@ -225,24 +231,23 @@
 
     def synthesize(c):
         arrivals(*first, c, send1_sem, recv1_sem).wait_recv()
-        right_high[pl.ds(0, coeffs)], right_low[pl.ds(0, coeffs)] = split(
-            recv1[c].reshape(coeffs, wide)
-        )
-        grid = dot3(
-            tall_high[...],
-            tall_low[...],
-            right_high[pl.ds(0, coeffs)],
-            right_low[pl.ds(0, coeffs)],
-        )
+        value = recv1[c].reshape(coeffs, wide)
+        even_k = lax.rem(count(value.shape, 0), 2) == 0
+        for side, part in enumerate((jnp.where(even_k, value, 0.0), jnp.where(even_k, 0.0, value))):
+            lanes = pl.ds(side * wide, wide)
+            right_high[:, lanes], right_low[:, lanes] = split(part)
+        both = dot3(tall_high[...], tall_low[...], right_high[...], right_low[...])
+        even_sum, odd_sum = both[:, :wide], both[:, wide:]
+        sums = 0.0
+        for side, grid in enumerate((even_sum + odd_sum, even_sum - odd_sum)):
+            here = pl.ds(side * fold, fold)
+            value = jnp.concatenate([gain[here]] * (wide // LANES), axis=1) * grid
+            product[c, here] = value
+            sums = sums + jnp.sum(value * value, axis=0, keepdims=True)
         for t in range(wide // LANES):
-            lanes = slice(t * LANES, (t + 1) * LANES)
-            value = gain[...] * grid[:, lanes]
-            product[c, :, lanes] = value
-            part_out[c, pl.ds(t, 1), :] = jnp.sum(value * value, axis=0, keepdims=True)
-
-        @pl.loop(1, n)
-        def _(k):
-            other = lax.rem(me + k, n)
+            part_out[c, pl.ds(t, 1), :] = sums[:, t * LANES : (t + 1) * LANES]
+
+        for other in others:
             pltpu.make_async_remote_copy(
                 src_ref=part_out.at[c],
                 dst_ref=part_in.at[c, me],
@@ -254,10 +259,10 @@
         part_in[c, me] = part_out[c]
 
     def analyze(c):
-        others = pl.ds(0, n - 1)
+        rest = pl.ds(0, n - 1)
         done = pltpu.make_async_remote_copy(
-            src_ref=part_in.at[c, others],
-            dst_ref=part_in.at[c, others],
+            src_ref=part_in.at[c, rest],
+            dst_ref=part_in.at[c, rest],
             send_sem=part_send_sem.at[c],
             recv_sem=part_recv_sem.at[c],
             device_id={"band": lax.rem(me + 1, n)},
@@ -274,12 +279,19 @@
             jnp.sum(jnp.where(left, 0.0, sums), axis=1, keepdims=True),
         )
         scale = 1.0 / jnp.sqrt(total * (1.0 / points) + 1e-06)
-        for t in range(wide // LANES):
-            lanes = slice(t * LANES, (t + 1) * LANES)
-            scaled = product[c, :, lanes] * scale[t : t + 1]
-            tendency = scaled + bend[...] * scaled * scaled
-            right_high[:, lanes], right_low[:, lanes] = split(tendency)
-        back = dot3(wide_high[...], wide_low[...], right_high[...], right_low[...])
+        scale = jnp.concatenate([scale[t : t + 1] for t in range(wide // LANES)], axis=1)
+        halves = []
+        for side in range(2):
+            here = pl.ds(side * fold, fold)
+            scaled = product[c, here] * scale
+            weight = jnp.concatenate([bend[here]] * (wide // LANES), axis=1)
+            halves.append(scaled + weight * scaled * scaled)
+        for side, part in enumerate((halves[0] + halves[1], halves[0] - halves[1])):
+            lanes = pl.ds(side * wide, wide)
+            down_high[:, lanes], down_low[:, lanes] = split(part)
+        both = dot3(wide_high[...], wide_low[...], down_high[...], down_low[...])
+        even_k = lax.rem(count((coeffs, wide), 0), 2) == 0
+        back = jnp.where(even_k, both[:, :wide], both[:, wide:])
         send2[c] = back.reshape(n, band, wide)
         send(*second, c, send2_sem, recv2_sem)
 
@@ -293,48 +305,58 @@
         arrivals(*second, c, send2_sem, recv2_sem).wait_recv()
         for level in range(0, GROUP, 2):
             place = pl.ds(level * rows, LANES)
-            for t in range(cells // LANES):
+            for t in range(fold // LANES):
                 lanes = pl.ds(t * LANES, LANES)
-                even = recv2[c, 2 * t, :, place]
-                odd = recv2[c, 2 * t + 1, :, place]
-                for which, value in (
-                    (level, jnp.where(low_half, even, pltpu.roll(odd, rows, 1))),
-                    (level + 1, jnp.where(low_half, pltpu.roll(even, rows, 1), odd)),
-                ):
-                    here = pl.ds(which * band, band)
-                    left_high[here, lanes], left_low[here, lanes] = split(value)
-        done = dot3(left_high[...], left_low[...], tall_high[...], tall_low[...])
+                turned = []
+                for near in (2 * t, 2 * t + fold // rows):
+                    even = recv2[c, near, :, place]
+                    odd = recv2[c, near + 1, :, place]
+                    turned.append(
+                        (
+                            jnp.where(low_half, even, pltpu.roll(odd, rows, 1)),
+                            jnp.where(low_half, pltpu.roll(even, rows, 1), odd),
+                        )
+                    )
+                for which in range(2):
+                    near, far = turned[0][which], turned[1][which]
+                    here = (level + which) * band
+                    for side, value in enumerate((near + far, near - far)):
+                        there = pl.ds(side * GROUP * band + here, band)
+                        left_high[there, lanes], left_low[there, lanes] = split(value)
+        both = dot3(left_high[...], left_low[...], tall_high[...], tall_low[...])
+        even_k = lax.rem(count((GROUP * band, coeffs), 1), 2) == 0
+        done = jnp.where(even_k, both[: GROUP * band], both[GROUP * band :])
         factor = weight(x_index) * weight(y_index) * (half / points)
         for level in range(GROUP):
             here = slice(level * band, (level + 1) * band)
             out[c, here, :] = done[here] * factor
 
-    @pl.loop(0, chunks + 3)
+    @pl.loop(0, chunks + FINISH)
     def _(t):
         @pl.when(t < chunks)
         def _():
             synthesize(t)
 
-        @pl.when(t + 2 < chunks)
-        def _():
-            send(*first, t + 2, send1_sem, recv1_sem)
-
-        @pl.when((t >= 1) & (t < chunks + 1))
-        def _():
-            analyze(t - 1)
-
-        @pl.when(t >= 3)
-        def _():
-            finish(t - 3)
+        @pl.when(t + AHEAD < chunks)
+        def _():
+            send(*first, t + AHEAD, send1_sem, recv1_sem)
+
+        @pl.when((t >= ANALYZE) & (t < chunks + ANALYZE))
+        def _():
+            analyze(t - ANALYZE)
+
+        @pl.when(t >= FINISH)
+        def _():
+            finish(t - FINISH)
 
     @pl.loop(0, chunks)
     def _(c):
         arrivals(*first, c, send1_sem, recv1_sem).wait_send()
         arrivals(*second, c, send2_sem, recv2_sem).wait_send()
-        others = pl.ds(0, n - 1)
+        rest = pl.ds(0, n - 1)
         pltpu.make_async_remote_copy(
-            src_ref=part_in.at[c, others],
-            dst_ref=part_in.at[c, others],
+            src_ref=part_in.at[c, rest],
+            dst_ref=part_in.at[c, rest],
             send_sem=part_send_sem.at[c],
             recv_sem=part_recv_sem.at[c],
             device_id={"band": lax.rem(me + 1, n)},
@@ -369,16 +391,18 @@
                 pltpu.VMEM((chunks, n, band, wide), F32),
                 pltpu.VMEM((chunks, wide // LANES, LANES), F32),
                 pltpu.VMEM((chunks, n, wide // LANES, LANES), F32),
-                pltpu.VMEM((coeffs, cells), BF16),
-                pltpu.VMEM((coeffs, cells), BF16),
-                pltpu.VMEM((cells, coeffs), BF16),
-                pltpu.VMEM((cells, coeffs), BF16),
+                pltpu.VMEM((coeffs, cells // 2), BF16),
+                pltpu.VMEM((coeffs, cells // 2), BF16),
+                pltpu.VMEM((cells // 2, coeffs), BF16),
+                pltpu.VMEM((cells // 2, coeffs), BF16),
                 pltpu.VMEM((cells, LANES), F32),
                 pltpu.VMEM((cells, LANES), F32),
-                pltpu.VMEM((GROUP * band, cells), BF16),
-                pltpu.VMEM((GROUP * band, cells), BF16),
-                pltpu.VMEM((cells, wide), BF16),
-                pltpu.VMEM((cells, wide), BF16),
+                pltpu.VMEM((2 * GROUP * band, cells // 2), BF16),
+                pltpu.VMEM((2 * GROUP * band, cells // 2), BF16),
+                pltpu.VMEM((coeffs, 2 * wide), BF16),
+                pltpu.VMEM((coeffs, 2 * wide), BF16),
+                pltpu.VMEM((cells // 2, 2 * wide), BF16),
+                pltpu.VMEM((cells // 2, 2 * wide), BF16),
             ]
             + [dma((chunks,)), dma((2,))] + [dma((chunks,))] * 6,
             compiler_params=pltpu.CompilerParams(

time: 80.7 us -> 78.7 us (0.975)
  Pallas kernels: 79.3 us -> 77.2 us
    pallas_call x1, Pallas kernels: 79.3 us -> 77.2 us  [on_device(): pl.pallas_call(functools.partial(kernel, n), out_shape=pltpu.VMEM((chunks...]
where the time goes in v2:
time: 78.7 us; the launch traced here: 78.6 us
  Pallas kernels  77.2 us (98%)
  local copies, waits for them, and re-layouts  1.41 us (2%)
    pallas_call x1, Pallas kernels, on_device(): pl.pallas_call(functools.partial(kernel, n), out_shape=pltpu.VMEM((chunks...  77.2 us

profile of v2, /device:TPU:1, one launch (start us, length us, event | category | flops | bytes accessed | tf_op | source)
XLA Modules:
  0.0 78.6 jit_solution(7589047601104704337)
XLA Ops:
  0.0 77.2 %shard_map.37 = f32[8,96,768]{2,1,0:T(8,128)S(1)} custom-call(f32[8,96,768]{2,1,0:T(8,128)} %bitcast.3, f32[64,1024]{1,0:T(8,128)} %coupling_hbm.1, f32[64,1024]{1,0:T(8,128)} %quadratic_hbm.1), custom_call_target="tpu_custom_call" | custom-call | tf_op jit(solution)/shard_map/pallas_call | solution.py:378
  77.2 1.4 %copy.5 = f32[16,48,768]{2,1,0:T(8,128)} copy(f32[16,48,768]{2,1,0:T(8,128)S(1)} %bitcast.2) | data formatting | bytes 4718592

commit v3 on v2

--- a/solution.py
+++ b/solution.py
@@ -16,7 +16,7 @@
 ANALYZE = 3
 FINISH = 6
 LANES = 128
-ORDER = ((1, 2), (0, 1), (1, 3), (0, 2), (1, 0), (0, 3), (1, 1), (0, 0))
+ORDER = ((1, 2), (0, 3), (1, 1), (0, 2), (1, 0), (0, 1), (1, 3), (0, 0))
 
 
 SINE = (-1.6666666666666666e-01, 8.3333333333333333e-03, -1.9841269841269841e-04, 2.7557319223985891e-06)
@@ -165,6 +165,17 @@
             device_id_type=MESH,
         )
 
+    def sums_of(c):
+        rest = pl.ds(0, n - 1)
+        return pltpu.make_async_remote_copy(
+            src_ref=part_in.at[c, rest],
+            dst_ref=part_in.at[c, rest],
+            send_sem=part_send_sem.at[c],
+            recv_sem=part_recv_sem.at[c],
+            device_id={"band": lax.rem(me + 1, n)},
+            device_id_type=MESH,
+        )
+
     first = (send1, recv1)
     second = (send2, recv2)
 
@@ -259,16 +270,7 @@
         part_in[c, me] = part_out[c]
 
     def analyze(c):
-        rest = pl.ds(0, n - 1)
-        done = pltpu.make_async_remote_copy(
-            src_ref=part_in.at[c, rest],
-            dst_ref=part_in.at[c, rest],
-            send_sem=part_send_sem.at[c],
-            recv_sem=part_recv_sem.at[c],
-            device_id={"band": lax.rem(me + 1, n)},
-            device_id_type=MESH,
-        )
-        done.wait_recv()
+        sums_of(c).wait_recv()
         sums = part_in[c, 0]
         for source in range(1, n):
             sums = sums + part_in[c, source]
@@ -302,6 +304,9 @@
         return jnp.where((index == 0) | (index == half), 1.0, 2.0)
 
     def finish(c):
+        arrivals(*first, c, send1_sem, recv1_sem).wait_send()
+        arrivals(*second, c, send2_sem, recv2_sem).wait_send()
+        sums_of(c).wait_send()
         arrivals(*second, c, send2_sem, recv2_sem).wait_recv()
         for level in range(0, GROUP, 2):
             place = pl.ds(level * rows, LANES)
@@ -348,20 +353,6 @@
         @pl.when(t >= FINISH)
         def _():
             finish(t - FINISH)
-
-    @pl.loop(0, chunks)
-    def _(c):
-        arrivals(*first, c, send1_sem, recv1_sem).wait_send()
-        arrivals(*second, c, send2_sem, recv2_sem).wait_send()
-        rest = pl.ds(0, n - 1)
-        pltpu.make_async_remote_copy(
-            src_ref=part_in.at[c, rest],
-            dst_ref=part_in.at[c, rest],
-            send_sem=part_send_sem.at[c],
-            recv_sem=part_recv_sem.at[c],
-            device_id={"band": lax.rem(me + 1, n)},
-            device_id_type=MESH,
-        ).wait_send()
 
 
 def solution(mesh):

time: 78.7 us -> 78.2 us (level)
  no operation moved by 1% of the time
where the time goes in v3:
time: 78.2 us
  Pallas kernels  76.7 us (98%)
  local copies, waits for them, and re-layouts  1.41 us (2%)
    pallas_call x1, Pallas kernels, on_device(): pl.pallas_call(functools.partial(kernel, n), out_shape=pltpu.VMEM((chunks...  76.7 us

profile of v3, /device:TPU:1, one launch (start us, length us, event | category | flops | bytes accessed | tf_op | source)
XLA Modules:
  0.0 78.2 jit_solution(1304998990758334264)
XLA Ops:
  0.0 76.7 %shard_map.37 = f32[8,96,768]{2,1,0:T(8,128)S(1)} custom-call(f32[8,96,768]{2,1,0:T(8,128)} %bitcast.3, f32[64,1024]{1,0:T(8,128)} %coupling_hbm.1, f32[64,1024]{1,0:T(8,128)} %quadratic_hbm.1), custom_call_target="tpu_custom_call" | custom-call | tf_op jit(solution)/shard_map/pallas_call | solution.py:369
  76.8 1.4 %copy.5 = f32[16,48,768]{2,1,0:T(8,128)} copy(f32[16,48,768]{2,1,0:T(8,128)S(1)} %bitcast.2) | data formatting | bytes 4718592

commit v4 on v3

--- a/solution.py
+++ b/solution.py
@@ -55,12 +55,45 @@
     return dot(a_high, b_high) + dot(a_low, b_high) + dot(a_high, b_low)
 
 
+def settle(both, me, band, points, start, coeffs):
+    rows, width = both.shape[0] // 2, both.shape[1]
+    half = coeffs // 2
+
+    def weight(index):
+        return jnp.where((index == 0) | (index == half), 1.0, 2.0)
+
+    y_index = lax.broadcasted_iota(jnp.int32, (rows, width), 1) + start
+    x_index = lax.rem(lax.broadcasted_iota(jnp.int32, (rows, width), 0), band) + me * band
+    done = jnp.where(lax.rem(y_index, 2) == 0, both[:rows], both[rows:])
+    return done * (weight(x_index) * weight(y_index) * (half / points))
+
+
+def last_kernel(band, points, ready, left_high, left_low, tall_high, tall_low, out, last, sem):
+    before, coeffs = ready.shape[0], ready.shape[2]
+    me = lax.axis_index("band")
+    copies = [pltpu.make_async_copy(ready, out.at[pl.ds(0, before)], sem.at[0])]
+    copies[0].start()
+    tile = 2 * LANES
+    for t in range(coeffs // tile):
+        lanes = pl.ds(t * tile, tile)
+        both = dot3(left_high[...], left_low[...], tall_high[:, lanes], tall_low[:, lanes])
+        last[t] = settle(both, me, band, points, t * tile, coeffs)
+        copies.append(pltpu.make_async_copy(last.at[t], out.at[before, :, lanes], sem.at[t + 1]))
+        copies[-1].start()
+    for copy in copies:
+        copy.wait()
+
+
 def kernel(
     n,
     spectral,
     coupling_hbm,
     quadratic_hbm,
     out,
+    left_high,
+    left_low,
+    tall_high,
+    tall_low,
     x_in,
     coupling,
     quadratic,
@@ -73,12 +106,8 @@
     part_in,
     wide_high,
     wide_low,
-    tall_high,
-    tall_low,
     gain,
     bend,
-    left_high,
-    left_low,
     right_high,
     right_low,
     down_high,
@@ -297,12 +326,6 @@
         send2[c] = back.reshape(n, band, wide)
         send(*second, c, send2_sem, recv2_sem)
 
-    x_index = lax.broadcasted_iota(jnp.int32, (band, coeffs), 0) + me * band
-    y_index = lax.broadcasted_iota(jnp.int32, (band, coeffs), 1)
-
-    def weight(index):
-        return jnp.where((index == 0) | (index == half), 1.0, 2.0)
-
     def finish(c):
         arrivals(*first, c, send1_sem, recv1_sem).wait_send()
         arrivals(*second, c, send2_sem, recv2_sem).wait_send()
@@ -328,13 +351,11 @@
                     for side, value in enumerate((near + far, near - far)):
                         there = pl.ds(side * GROUP * band + here, band)
                         left_high[there, lanes], left_low[there, lanes] = split(value)
-        both = dot3(left_high[...], left_low[...], tall_high[...], tall_low[...])
-        even_k = lax.rem(count((GROUP * band, coeffs), 1), 2) == 0
-        done = jnp.where(even_k, both[: GROUP * band], both[GROUP * band :])
-        factor = weight(x_index) * weight(y_index) * (half / points)
-        for level in range(GROUP):
-            here = slice(level * band, (level + 1) * band)
-            out[c, here, :] = done[here] * factor
+
+        @pl.when(c < chunks - 1)
+        def _():
+            both = dot3(left_high[...], left_low[...], tall_high[...], tall_low[...])
+            out[c] = settle(both, me, band, points, 0, coeffs)
 
     @pl.loop(0, chunks + FINISH)
     def _(t):
@@ -366,11 +387,17 @@
         dma = pltpu.SemaphoreType.DMA
         vmem = pl.BlockSpec(memory_space=pltpu.VMEM)
         hbm = pl.BlockSpec(memory_space=pltpu.HBM)
-        result = pl.pallas_call(
+        parts = pl.pallas_call(
             functools.partial(kernel, n),
-            out_shape=pltpu.VMEM((chunks, GROUP * band, coeffs), F32),
+            out_shape=(
+                pltpu.VMEM((chunks - 1, GROUP * band, coeffs), F32),
+                pltpu.VMEM((2 * GROUP * band, cells // 2), BF16),
+                pltpu.VMEM((2 * GROUP * band, cells // 2), BF16),
+                pltpu.VMEM((cells // 2, coeffs), BF16),
+                pltpu.VMEM((cells // 2, coeffs), BF16),
+            ),
             in_specs=[hbm] * 3,
-            out_specs=vmem,
+            out_specs=(vmem,) * 5,
             scratch_shapes=[
                 pltpu.VMEM((chunks, GROUP * band, coeffs), F32),
                 pltpu.VMEM((rows, cells), F32),
@@ -384,12 +411,8 @@
                 pltpu.VMEM((chunks, n, wide // LANES, LANES), F32),
                 pltpu.VMEM((coeffs, cells // 2), BF16),
                 pltpu.VMEM((coeffs, cells // 2), BF16),
-                pltpu.VMEM((cells // 2, coeffs), BF16),
-                pltpu.VMEM((cells // 2, coeffs), BF16),
                 pltpu.VMEM((cells, LANES), F32),
                 pltpu.VMEM((cells, LANES), F32),
-                pltpu.VMEM((2 * GROUP * band, cells // 2), BF16),
-                pltpu.VMEM((2 * GROUP * band, cells // 2), BF16),
                 pltpu.VMEM((coeffs, 2 * wide), BF16),
                 pltpu.VMEM((coeffs, 2 * wide), BF16),
                 pltpu.VMEM((cells // 2, 2 * wide), BF16),
@@ -405,6 +428,17 @@
                 for value in (spectral.reshape(chunks, GROUP * band, coeffs), coupling, quadratic)
             )
         )
+        result = pl.pallas_call(
+            functools.partial(last_kernel, band, float(cells * cells)),
+            out_shape=jax.ShapeDtypeStruct((chunks, GROUP * band, coeffs), F32),
+            in_specs=[vmem] * 5,
+            out_specs=pl.BlockSpec(memory_space=pltpu.HBM),
+            scratch_shapes=[
+                pltpu.VMEM((coeffs // (2 * LANES), GROUP * band, 2 * LANES), F32),
+                dma((1 + coeffs // (2 * LANES),)),
+            ],
+            compiler_params=pltpu.CompilerParams(vmem_limit_bytes=16 * 1024 * 1024),
+        )(*(pltpu.with_memory_space_constraint(part, pltpu.VMEM) for part in parts))
         return result.reshape(levels, band, coeffs)
 
     spec = P("member", "band", None)

time: 78.2 us -> 77.7 us (level)
  local copies, waits for them, and re-layouts: 1.41 us -> 0 us
  Pallas kernels: 76.7 us -> 77.6 us
    unnamed x1 -> x0, local copies, waits for them, and re-layouts: 1.41 us -> none
    pallas_call x1 -> x2, Pallas kernels: 76.7 us -> 77.6 us  [the longest x1 76.2 us: on_device(): pl.pallas_call(functools.partial(kernel, n), out_shape=(pltpu.VMEM((chunk...]
where the time goes in v4:
time: 77.7 us; the launch traced here: 77.6 us
  Pallas kernels  77.6 us (100%)
    pallas_call x1, Pallas kernels, on_device(): pl.pallas_call(functools.partial(kernel, n), out_shape=(pltpu.VMEM((chunk...  76.2 us

profile of v4, /device:TPU:1, one launch (start us, length us, event | category | flops | bytes accessed | tf_op | source)
XLA Modules:
  0.0 77.6 jit_solution(18200606907884884431)
XLA Ops:
  0.0 76.2 %shard_map.37 = (f32[7,96,768]{2,1,0:T(8,128)S(1)}, bf16[192,512]{1,0:T(8,128)(2,1)S(1)}, bf16[192,512]{1,0:T(8,128)(2,1)S(1)}, bf16[512,768]{1,0:T(8,128)(2,1)S(1)}, bf16[512,768]{1,0:T(8,128)(2,1)S(1)}) custom-call(f32[8,96,768]{2,1,0:T(8,128)} %bitcast.2, f32[64,1024]{1,0:T(8,128)} %coupling_hbm.1, f32[64,1024]{1,0:T(8,128)} %quadratic_hbm.1), custom_call_target="tpu_custom_call" | custom-call | tf_op jit(solution)/shard_map/pallas_call | solution.py:390
  76.2 1.4 %shard_map.38 = f32[8,96,768]{2,1,0:T(8,128)} custom-call(f32[7,96,768]{2,1,0:T(8,128)S(1)} %get-tuple-element.10.ready, bf16[192,512]{1,0:T(8,128)(2,1)S(1)} %get-tuple-element.11.left_high, bf16[192,512]{1,0:T(8,128)(2,1)S(1)} %get-tuple-element.12.left_low, bf16[512,768]{1,0:T(8,128)(2,1)S(1)} %get-tuple-element.13.tall_high, ...), custom_call_target="tpu_custom_call" | custom-call | tf_op jit(solution)/shard_map/pallas_call | solution.py:431

commit v5 on v4

--- a/solution.py
+++ b/solution.py
@@ -16,7 +16,7 @@
 ANALYZE = 3
 FINISH = 6
 LANES = 128
-ORDER = ((1, 2), (0, 3), (1, 1), (0, 2), (1, 0), (0, 1), (1, 3), (0, 0))
+ORDER = ((1, 1), (0, 3), (1, 2), (0, 1), (1, 3), (0, 2), (1, 0), (0, 0))
 
 
 SINE = (-1.6666666666666666e-01, 8.3333333333333333e-03, -1.9841269841269841e-04, 2.7557319223985891e-06)

time: 77.7 us -> 77.5 us (level)
  no operation moved by 1% of the time
where the time goes in v5:
time: 77.5 us; the launch traced here: 77.4 us
  Pallas kernels  77.4 us (100%)
    pallas_call x1, Pallas kernels, on_device(): pl.pallas_call(functools.partial(kernel, n), out_shape=(pltpu.VMEM((chunk...  75.9 us

profile of v5, /device:TPU:1, one launch (start us, length us, event | category | flops | bytes accessed | tf_op | source)
XLA Modules:
  0.0 77.4 jit_solution(15575226136653277271)
XLA Ops:
  0.0 75.9 %shard_map.37 = (f32[7,96,768]{2,1,0:T(8,128)S(1)}, bf16[192,512]{1,0:T(8,128)(2,1)S(1)}, bf16[192,512]{1,0:T(8,128)(2,1)S(1)}, bf16[512,768]{1,0:T(8,128)(2,1)S(1)}, bf16[512,768]{1,0:T(8,128)(2,1)S(1)}) custom-call(f32[8,96,768]{2,1,0:T(8,128)} %bitcast.2, f32[64,1024]{1,0:T(8,128)} %coupling_hbm.1, f32[64,1024]{1,0:T(8,128)} %quadratic_hbm.1), custom_call_target="tpu_custom_call" | custom-call | tf_op jit(solution)/shard_map/pallas_call | solution.py:390
  76.0 1.4 %shard_map.38 = f32[8,96,768]{2,1,0:T(8,128)} custom-call(f32[7,96,768]{2,1,0:T(8,128)S(1)} %get-tuple-element.10.ready, bf16[192,512]{1,0:T(8,128)(2,1)S(1)} %get-tuple-element.11.left_high, bf16[192,512]{1,0:T(8,128)(2,1)S(1)} %get-tuple-element.12.left_low, bf16[512,768]{1,0:T(8,128)(2,1)S(1)} %get-tuple-element.13.tall_high, ...), custom_call_target="tpu_custom_call" | custom-call | tf_op jit(solution)/shard_map/pallas_call | solution.py:431
